TPU v7x, 32 devices: a whole 2x2x4 slice. The times are simulated.
32 devices in a mesh: dp: 16 (over z, y, x), mp: 2 (over core).
Axes of the slice: x: 2, y: 2, z: 4, core: 2. Of those that a mesh axis runs over, the one named last changes fastest.
Arguments:
- points: bfloat16 [16384, 1024], P(('dp', 'mp')), may hold values from -6 to 6
- centroids: bfloat16 [4096, 1024], P('mp'), may hold values from -6 to 6
- assign: int32 [16384], P(('dp', 'mp')), may hold values from 0 to 4095
- keep_mask: int32 [16384], P(('dp', 'mp')), may hold values 0 or 1
Outputs:
- new_centroids: float32 [4096, 1024], P('mp')
- row_cost: float32 [16384], P(('dp', 'mp'))
All inputs are finite; a program needn't handle non-finite values. No bound on the sum of `keep_mask` on one device may be relied on, other than what follows from the above.
Results may differ from a plain program's by a relative error of at most 0.0008.
Values may be sent and summed in bfloat16 or wider, within the bound.
A program may use at most 128 MiB of HBM per device.

v0:
```python
import functools

import jax
import jax.numpy as jnp
from jax import lax
from jax.experimental import pallas as pl
from jax.experimental.pallas import tpu as pltpu
from jax.sharding import Mesh
from jax.sharding import PartitionSpec as P

STEPS = 32000.0
TINY = 2.0**-100
EXTRA = 8
PLANE = 4
LANES = 128
CHUNKS = 2
MESH = pl.DeviceIdType.MESH


def remote(src, dst, send, recv, device):
    return pltpu.make_async_remote_copy(
        src_ref=src, dst_ref=dst, send_sem=send, recv_sem=recv, device_id=device, device_id_type=MESH
    )


def update_kernel(
    z_n, shard_rows, p_ref, id_ref, prior_ref, c_ref, out_ref, low_ref,
    crecv, near, idn, acc, mrecv, red, zright,
    cs, cr, ids_s, ids_r, ps, pr, ms, mr, rs, rr,
    grs, grr, gls, glr, xs, xr, ys, yr, ds_, dr,
):
    z, q, m = lax.axis_index("z"), lax.axis_index("q"), lax.axis_index("mp")
    nx = q + 1 - 2 * lax.rem(q, 2)
    ny = lax.rem(q + 2, PLANE)
    nd = ny + 1 - 2 * lax.rem(ny, 2)
    other = 1 - m
    rows, width = p_ref.shape
    block = prior_ref.shape[0]
    half = rows // 2
    part = width // CHUNKS
    code_w = part // 2
    last = z_n - 1
    up, down = lax.rem(z + 1, z_n), lax.rem(z + last, z_n)

    barrier = pltpu.get_barrier_semaphore()
    peers = [(z, nx, m), (z, ny, m), (z, nd, m), (z, q, other)]
    peers += [(lax.rem(z + k, z_n), q, m) for k in range(1, z_n)]
    for peer in peers:
        pl.semaphore_signal(barrier, inc=1, device_id=peer, device_id_type=MESH)
    pl.semaphore_wait(barrier, len(peers))

    id_copies = [
        remote(id_ref, idn.at[k], ids_s.at[k], ids_r.at[k], (z, to, m))
        for k, to in enumerate((nx, ny, nd))
    ]
    lo, hi = pl.ds(0, half), pl.ds(half, half)

    def gather_copies(c):
        cols = pl.ds(c * part, part)

        def piece(k, src, slot, span, to):
            return remote(src, near.at[c, slot, span], ps.at[c, k], pr.at[c, k], (z, to, m))

        return (
            piece(0, p_ref.at[lo, cols], 0, lo, nx),
            piece(1, p_ref.at[hi, cols], 1, hi, ny),
            piece(2, p_ref.at[hi, cols], 0, hi, nx),
            piece(3, p_ref.at[lo, cols], 1, lo, ny),
            piece(4, near.at[c, 0, lo], 2, lo, ny),
            piece(5, near.at[c, 1, hi], 2, hi, nx),
        )

    gathers = [gather_copies(c) for c in range(CHUNKS)]

    def width_of(c):
        return part + (LANES if c == 0 else 0)

    def add(c, ids, pts, first):
        def tile(t, carry):
            base = (t // z_n) * shard_rows + (lax.rem(t, z_n) * PLANE + q) * block
            row = base + lax.broadcasted_iota(jnp.int32, (block, rows), 0)
            hit = jnp.where(row == ids[0:1, :], 1.0, 0.0)
            s = jnp.dot(hit.astype(jnp.bfloat16), pts[...], preferred_element_type=jnp.float32)
            if first:
                acc[c, t, :, :part] = s
            else:
                acc[c, t, :, :part] += s
            if c == 0:
                count = jnp.broadcast_to(jnp.sum(hit, axis=1, keepdims=True), (block, LANES))
                if first:
                    acc[c, t, :, part:] = count
                else:
                    acc[c, t, :, part:] += count
            return carry

        lax.fori_loop(0, 2 * z_n, tile, 0)

    ctile = 256

    def lowest(cents, first):
        def tile(t, best):
            tile_ref = cents[pl.ds(pl.multiple_of(t * ctile, ctile), ctile), :]
            wide = tile_ref.astype(jnp.float32)
            sq = jnp.sum(wide * wide, axis=1, keepdims=True)
            inner = lax.dot_general(
                tile_ref, p_ref[...], (((1,), (1,)), ((), ())), preferred_element_type=jnp.float32
            )
            return jnp.minimum(best, jnp.min(sq - 2.0 * inner, axis=0, keepdims=True))

        start = jnp.full((1, rows), jnp.inf, jnp.float32) if first else low_ref[0:1, :]
        best = lax.fori_loop(0, shard_rows // ctile, tile, start)
        low_ref[...] = jnp.broadcast_to(best, low_ref.shape)

    ccopy = remote(c_ref, crecv, cs, cr, (z, q, other))
    for copy in id_copies + list(gathers[0][:4]):
        copy.start()
    ccopy.start()

    mcopies = []

    def open_gather(c):
        a, b2, _, _, e, f = gathers[c]
        add(c, id_ref, p_ref.at[:, pl.ds(c * part, part)], True)
        a.wait_recv()
        e.start()
        b2.wait_recv()
        f.start()
        if c + 1 < CHUNKS:
            for copy in gathers[c + 1][:4]:
                copy.start()

    def close_gather(c):
        _, _, b, d, e, f = gathers[c]
        if c == 0:
            lowest(c_ref, True)
            for copy in id_copies:
                copy.wait_recv()
        b.wait_recv()
        add(c, idn.at[0], near.at[c, 0], False)
        d.wait_recv()
        add(c, idn.at[1], near.at[c, 1], False)
        if c == 0:
            ccopy.wait_recv()
            lowest(crecv, False)
        e.wait_recv()
        f.wait_recv()
        add(c, idn.at[2], near.at[c, 2], False)
        w = pl.ds(0, width_of(c))
        copy = remote(
            acc.at[c, pl.ds(other * z_n, z_n), :, w], mrecv.at[c, :, :, w],
            ms.at[c], mr.at[c], (z, q, other),
        )
        copy.start()
        mcopies.append(copy)

    def direct(c, k):
        w = pl.ds(0, width_of(c))
        to = lax.rem(z + k, z_n)
        return remote(
            red.at[c, to, :, w], zright.at[c, k, :, w], rs.at[c, k], rr.at[c, k], (to, q, m)
        )

    def combine(c):
        mcopies[c].wait_recv()
        w = width_of(c)
        for k in range(1, z_n + 1):
            t = lax.rem(z + k, z_n)
            red[c, t, :, :w] = acc[c, m * z_n + t, :, :w] + mrecv[c, t, :, :w]
            if k < z_n:
                direct(c, k).start()

    own = z * PLANE + q

    def xcopy(c, n, to_q):
        at = out_ref.at[c, n * PLANE + to_q]
        return remote(at, at, xs.at[c, n], xr.at[c, n], (z, nx, m))

    def ycopy(c, n, to_q):
        at = out_ref.at[c, n * PLANE + to_q]
        return remote(at, at, ys.at[c, n], yr.at[c, n], (z, ny, m))

    def dcopy(c, n, by_x):
        at = out_ref.at[c, n * PLANE + (nx if by_x else ny)]
        return remote(at, at, ds_.at[c, n], dr.at[c, n], (z, ny if by_x else nx, m))

    def gright(c, n):
        at = out_ref.at[c, n * PLANE + q]
        return remote(at, at, grs.at[c, n], grr.at[c, n], (up, q, m))

    def gleft(c, n):
        at = out_ref.at[c, n * PLANE + q]
        return remote(at, at, gls.at[c, n], glr.at[c, n], (down, q, m))

    def publish(c, count):
        w = width_of(c)

        for k in range(1, z_n):
            direct(c, k).wait_recv()
            red[c, z, :, :w] += zright[c, k, :, :w]

        if c == 0:
            count = red[c, z, :, part : part + 1]
        prior = prior_ref[:, c * part : (c + 1) * part].astype(jnp.float32)
        fresh = jnp.where(count > 0.5, red[c, z, :, :part] / jnp.maximum(count, 1.0), prior)
        top = jnp.max(jnp.abs(fresh), axis=1, keepdims=True)
        power = jnp.ceil(jnp.log2(jnp.maximum(top, TINY)))
        code = jnp.floor(fresh * jnp.exp2(-power) * STEPS + 0.5).astype(jnp.int32)
        out_ref[c, own, :block] = (code[:, :code_w] << 16) | (code[:, code_w:] & 0xFFFF)
        at_row = lax.broadcasted_iota(jnp.int32, (block, LANES), 0)
        at_lane = lax.broadcasted_iota(jnp.int32, (block, LANES), 1)
        flat = jnp.sum(jnp.where(at_row == at_lane, power, 0.0), axis=0, keepdims=True)
        out_ref[c, own, block:] = jnp.zeros((EXTRA, code_w), jnp.int32)
        out_ref[c, own, block:, :LANES] = jnp.broadcast_to(flat.astype(jnp.int32), (EXTRA, LANES))

        @pl.when(z < last)
        def _(c=c):
            gright(c, z).start()

        @pl.when(z > 0)
        def _(c=c):
            gleft(c, z).start()

        xcopy(c, z, q).start()
        ycopy(c, z, q).start()
        return count

    def relay(c, n, by_x):
        if by_x:
            xcopy(c, n, nx).wait_recv()
        else:
            ycopy(c, n, ny).wait_recv()
        dcopy(c, n, by_x).start()

    def settle(c, n, by_x):
        if by_x:
            ycopy(c, n, ny).wait_recv()
        else:
            xcopy(c, n, nx).wait_recv()
        dcopy(c, n, by_x).wait_recv()

    def each(k, c, action):
        if k == 0:
            action(c, z, c % 2 == 0)
            return

        @pl.when(z >= k)
        def _():
            action(c, z - k, k % 2 == 0)

        @pl.when(z + k <= last)
        def _():
            action(c, z + k, k % 2 == 1)

    def spread(c, k):
        @pl.when(z >= k)
        def _():
            gright(c, z - k).wait_recv()

            @pl.when(z < last)
            def _():
                gright(c, z - k).start()

            xcopy(c, z - k, q).start()
            ycopy(c, z - k, q).start()

        @pl.when(z + k <= last)
        def _():
            gleft(c, z + k).wait_recv()

            @pl.when(z > 0)
            def _():
                gleft(c, z + k).start()

            xcopy(c, z + k, q).start()
            ycopy(c, z + k, q).start()

        each(k - 1, c, relay)

    open_gather(0)
    close_gather(0)
    for c in range(CHUNKS):
        if c + 1 < CHUNKS:
            open_gather(c + 1)
        combine(c)
        if c + 1 < CHUNKS:
            close_gather(c + 1)
    count = None
    for c in range(CHUNKS):
        count = publish(c, count)
    for k in range(1, z_n):
        for c in range(CHUNKS):
            spread(c, k)
    for c in range(CHUNKS):
        each(last, c, relay)
    for k in range(z_n):
        for c in range(CHUNKS):
            each(k, c, settle)

    for copy in id_copies + [ccopy] + mcopies:
        copy.wait_send()
    for c in range(CHUNKS):
        for copy in gathers[c]:
            copy.wait_send()
        for t in range(z_n):

            if t > 0:
                direct(c, t).wait_send()

            @pl.when((z >= t) & (z < last))
            def _(c=c, t=t):
                gright(c, t).wait_send()

            @pl.when((z <= t) & (z > 0))
            def _(c=c, t=t):
                gleft(c, t).wait_send()

            xcopy(c, t, q).wait_send()
            ycopy(c, t, q).wait_send()
            dcopy(c, t, True).wait_send()


def shards(points, centroids, assign, keep_mask):
    rows, width = points.shape
    shard_rows = centroids.shape[0]
    z_n = lax.axis_size("z")
    dp_n = z_n * PLANE
    block = shard_rows // dp_n
    own = lax.axis_index("z") * PLANE + lax.axis_index("q")
    ids = jnp.where(keep_mask > 0, assign, -1)
    ids = jnp.broadcast_to(ids[None, :], (8, rows))
    prior = lax.dynamic_slice_in_dim(centroids, own * block, block, 0)
    vmem = pl.BlockSpec(memory_space=pltpu.VMEM)
    dma = pltpu.SemaphoreType.DMA
    part = width // CHUNKS
    wide = part + LANES
    per = dma((CHUNKS, z_n))
    back, low = pl.pallas_call(
        functools.partial(update_kernel, z_n, shard_rows),
        out_shape=(
            jax.ShapeDtypeStruct((CHUNKS, dp_n, block + EXTRA, part // 2), jnp.int32),
            jax.ShapeDtypeStruct((8, rows), jnp.float32),
        ),
        in_specs=[vmem] * 4,
        out_specs=(vmem, vmem),
        scratch_shapes=[
            pltpu.VMEM((shard_rows, width), centroids.dtype),
            pltpu.VMEM((CHUNKS, 3, rows, part), points.dtype),
            pltpu.VMEM((3, 8, rows), jnp.int32),
            pltpu.VMEM((CHUNKS, 2 * z_n, block, wide), jnp.float32),
            pltpu.VMEM((CHUNKS, z_n, block, wide), jnp.float32),
            pltpu.VMEM((CHUNKS, z_n, block, wide), jnp.float32),
            pltpu.VMEM((CHUNKS, z_n, block, wide), jnp.float32),
            dma, dma, dma((3,)), dma((3,)), dma((CHUNKS, 6)), dma((CHUNKS, 6)),
            dma((CHUNKS,)), dma((CHUNKS,)),
            per, per, per, per, per, per, per, per, per, per, per, per,
        ],
        compiler_params=pltpu.CompilerParams(
            collective_id=0, has_side_effects=True, vmem_limit_bytes=56 * 1024 * 1024
        ),
        cost_estimate=pl.CostEstimate(
            flops=0, bytes_accessed=200 * 1024 * 1024, transcendentals=0
        ),
    )(points, ids, prior, centroids)
    codes = back[:, :, :block]
    powers = back[:, :, block, :block].astype(jnp.float32)
    scale = (jnp.exp2(powers) / STEPS)[:, :, :, None]
    pieces = []
    for c in range(CHUNKS):
        pieces += [(codes[c] >> 16) * scale[c], ((codes[c] << 16) >> 16) * scale[c]]
    new_centroids = jnp.concatenate(pieces, axis=2).reshape(shard_rows, width)
    point_f = points.astype(jnp.float32)
    point_sq = jnp.sum(point_f * point_f, axis=1)
    return new_centroids, (point_sq + low[0]) / width


def solution(mesh):
    dp, mp = mesh.shape["dp"], mesh.shape["mp"]
    grid = Mesh(mesh.devices.reshape(dp // PLANE, PLANE, mp), ("z", "q", "mp"))
    rows = ("z", "q", "mp")
    in_specs = (P(rows, None), P("mp", None), P(rows), P(rows))
    out_specs = (P("mp", None), P(rows))
    return jax.shard_map(shards, mesh=grid, in_specs=in_specs, out_specs=out_specs, check_vma=False)
```

profile of v0, /device:TPU:0, one launch (start us, length us, event | category | flops | bytes accessed | tf_op | source)
XLA Modules:
  0.0 140.8 jit_solution(10201832552461841946)
XLA Ops:
  0.6 0.7 compare_select_fusion
  1.3 1.5 %multiply_reduce_fusion = f32[512]{0:T(512)S(1)} fusion(bf16[512,1024]{1,0:T(8,128)(2,1)} %p_ref.1), kind=kLoop, calls=%fused_computation.5 | loop fusion | flops 1572352 | bytes 1050624 | tf_op jit(solution)/shard_map/reduce_sum | solution.py:372
  2.8 0.6 broadcast_in_dim.12.id_ref
  3.4 1.7 %constant_dynamic-slice_fusion.prior_ref = bf16[128,1024]{1,0:T(8,128)(2,1)} fusion(bf16[2048,1024]{1,0:T(8,128)(2,1)} %c_ref.1, s32[]{:T(128)S(6)} %select_n.8), kind=kLoop, calls=%fused_computation.13 | loop fusion | bytes 524292 | tf_op jit(solution)/shard_map/dynamic_slice | solution.py:331
  5.1 124.7 %shard_map.59 = (s32[2,16,136,256]{3,2,1,0:T(8,128)}, f32[8,512]{1,0:T(8,128)}) custom-call(bf16[512,1024]{1,0:T(8,128)(2,1)} %p_ref.1, s32[8,512]{1,0:T(8,128)} %broadcast_in_dim.12.id_ref, bf16[128,1024]{1,0:T(8,128)(2,1)} %constant_dynamic-slice_fusion.prior_ref, bf16[2048,1024]{1,0:T(8,128)(2,1)} %c_ref.1), custom_call_target="tpu_custom_call" | custom-call | bytes 209715200 | tf_op jit(solution)/shard_map/pallas_call | solution.py:337
  129.9 0.7 slice.34
  130.6 0.6 add_multiply_fusion
  131.2 0.9 exponential_multiply_fusion
  132.1 3.4 %shift-right-arithmetic_convert_fusion.3 = (f32[1,16,128,256]{3,2,1,0:T(8,128)S(1)}, f32[1,16,128,256]{3,2,1,0:T(8,128)S(1)}, f32[1,16,128,256]{3,2,1,0:T(8,128)S(1)}, f32[1,16,128,256]{3,2,1,0:T(8,128)S(1)}) fusion(s32[2,16,136,256]{3,2,1,0:T(8,128)} %get-tuple-element.4), kind=kLoop, calls=%fused_computation.9 | loop fusion | flops 5242880 | bytes 12582912 | tf_op jit(solution)/shard_map/convert_element_type | solution.py:369
  135.5 1.3 bitcast_multiply_fusion.1
  136.8 4.1 %pad_maximum_fusion = f32[2048,1024]{1,0:T(8,128)} fusion(f32[2048,256]{1,0:T(8,128)S(1)} %get-tuple-element.15, f32[2048,256]{1,0:T(8,128)S(1)} %get-tuple-element.14, f32[2048,256]{1,0:T(8,128)S(1)} %get-tuple-element.16, f32[2048,256]{1,0:T(8,128)S(1)} %get-tuple-element.17), kind=kLoop, calls=%fused_computation | loop fusion | flops 6291456 | bytes 16777216 | tf_op jit(solution)/shard_map/concatenate | solution.py:370
  (1 shorter events, 0.0 us)
where the time goes:
time: 143 us; the launch traced here: 141 us
  Pallas kernels  125 us (87%)
  other arithmetic  12.4 us (9%)
  local copies, waits for them, and re-layouts  2.99 us (2%)
    pallas_call x1, Pallas kernels, shards(): pl.pallas_call(functools.partial(update_kernel, z_n, shard_rows), out_sha...  125 us
    concatenate x1, other arithmetic, shards(): new_centroids = jnp.concatenate(pieces, axis=2).reshape(shard_rows, width)  4.06 us
    convert_element_type x1, other arithmetic, shards(): pieces += [(codes[c] >> 16) * scale[c], (codes[c] << 16 >> 16) * scale[c]]  3.37 us

commit v1 on v0

v1 whole, which is shorter than its diff:
```python
import functools

import jax
import jax.numpy as jnp
from jax import lax
from jax.experimental import pallas as pl
from jax.experimental.pallas import tpu as pltpu
from jax.sharding import Mesh
from jax.sharding import PartitionSpec as P

STEPS = 32000.0
TINY = 2.0**-100
BIAS = 128
WORD = 24
PLANE = 4
LANES = 128
CTILE = 256
MESH = pl.DeviceIdType.MESH


def remote(src, dst, send, recv, device):
    return pltpu.make_async_remote_copy(
        src_ref=src, dst_ref=dst, send_sem=send, recv_sem=recv, device_id=device, device_id_type=MESH
    )


def power_of(top):
    return jnp.ceil(jnp.log2(jnp.maximum(top, TINY)))


def quantize(v, power):
    return jnp.floor(v * (jnp.exp2(-power) * STEPS) + 0.5).astype(jnp.int32)


def embed(code, word):
    lane = lax.broadcasted_iota(jnp.int32, code.shape, 1)
    bit = lax.shift_right_logical(jnp.broadcast_to(word, code.shape), jnp.minimum(lane, 31)) & 1
    return (code & jnp.where(lane < WORD, -2, -1)) | bit


def pack(code):
    half = code.shape[0] // 2
    return (code[:half] << 16) | (code[half:] & 0xFFFF)


def unpack(packed):
    return jnp.concatenate([packed >> 16, (packed << 16) >> 16], axis=0)


def word_of(code):
    lane = lax.broadcasted_iota(jnp.int32, (1, LANES), 1)
    weight = jnp.where(lane < WORD, 1 << jnp.minimum(lane, WORD), 0).astype(jnp.float32)
    return jnp.sum((code & 1).astype(jnp.float32) * weight, axis=1, keepdims=True).astype(jnp.int32)


def scale_of(word):
    return jnp.exp2(((word & 255) - BIAS).astype(jnp.float32)) / STEPS


def encode(v, count=None):
    power = power_of(jnp.max(jnp.abs(v), axis=1, keepdims=True))
    word = power.astype(jnp.int32) + BIAS
    if count is not None:
        word = word + (count.astype(jnp.int32) << 8)
    return pack(embed(quantize(v, power), word))


def decode(packed):
    code = unpack(packed)
    word = word_of(code)
    return code.astype(jnp.float32) * scale_of(word), (word >> 8).astype(jnp.float32)


def update_kernel(
    z_n, pairs, p_hbm, c_hbm, assign_ref, keep_ref, out_ref, cost_ref,
    p2, cents, prior, idv, slot, hit, pn, acc, cnt, asend, arecv, zsend, zrecv, low, lowr,
    loc, ids_s, ids_r, mt_s, mt_r, ps, pr, fs, fr, as_, ar, zs, zr,
    grs, grr, gls, glr, xs, xr, ys, yr, ds_, dr, lo_s, lo_r,
):
    z, q, m = lax.axis_index("z"), lax.axis_index("q"), lax.axis_index("mp")
    nx = q + 1 - 2 * lax.rem(q, 2)
    ny = lax.rem(q + 2, PLANE)
    other = 1 - m
    rows, width = p_hbm.shape
    shard_rows = c_hbm.shape[0]
    block = prior.shape[0]
    both = 2 * rows
    kept = z_n * block
    side_w = width // 2
    part = side_w // pairs
    last = z_n - 1
    up, down = lax.rem(z + 1, z_n), lax.rem(z + last, z_n)
    own = z * PLANE + q
    near, far = (nx, ny), (ny, nx)

    load_p = pltpu.make_async_copy(p_hbm, p2.at[pl.ds(0, rows)], loc.at[0])
    load_prior = pltpu.make_async_copy(
        c_hbm.at[pl.ds(pl.multiple_of(own * block, block), block)], prior, loc.at[1]
    )
    load_c = pltpu.make_async_copy(c_hbm, cents, loc.at[2])
    load_p.start()
    idv[0] = jnp.where(keep_ref[...] > 0, assign_ref[...], -1)

    barrier = pltpu.get_barrier_semaphore()
    peers = [(z, q, other), (z, nx, m), (z, nx, other), (z, ny, m), (z, ny, other)]
    greet = peers + [(lax.rem(z + k, z_n), q, m) for k in range(1, z_n)]
    for peer in greet:
        pl.semaphore_signal(barrier, inc=1, device_id=peer, device_id_type=MESH)
    load_c.start()
    load_prior.start()
    pl.semaphore_wait(barrier, len(greet))

    def pts_copy(s, p):
        cols = pl.ds(s * side_w + p * part, part)
        return remote(
            p2.at[pl.ds(0, rows), cols], pn.at[s, p, pl.ds(0, rows)], ps.at[s, p], pr.at[s, p],
            (z, near[s], m),
        )

    def fwd_copy(s, p):
        return remote(
            pn.at[s, p, pl.ds(0, rows)], pn.at[s, p, pl.ds(rows, rows)], fs.at[s, p], fr.at[s, p],
            (z, q, other),
        )

    def a_copy(s, p):
        return remote(asend.at[s, p], arecv.at[s, p], as_.at[s, p], ar.at[s, p], (z, far[s], m))

    def z_copy(p, k):
        to = lax.rem(z + k, z_n)
        return remote(zsend.at[p, to], zrecv.at[p, k], zs.at[p, k], zr.at[p, k], (to, q, m))

    id_copies = [
        remote(idv.at[0], idv.at[k + 1], ids_s.at[k], ids_r.at[k], peer) for k, peer in enumerate(peers)
    ]
    mate_copy = remote(p2.at[pl.ds(0, rows)], p2.at[pl.ds(rows, rows)], mt_s, mt_r, (z, q, other))

    load_p.wait()
    for copy in id_copies:
        copy.start()
    for s in range(2):
        pts_copy(s, 0).start()
    mate_copy.start()
    for p in range(1, pairs - 1):
        for s in range(2):
            pts_copy(s, p).start()
    for copy in id_copies:
        copy.wait_recv()

    def slots_of(s, a, b):
        ids = jnp.concatenate([idv[a], idv[b]], axis=1) - m * shard_rows
        inside = (ids >= 0) & (ids < shard_rows)
        ids = jnp.where(inside, ids, 0)
        owner = lax.rem(lax.div(ids, block), PLANE)
        at = lax.div(ids, block * PLANE) * block + lax.rem(ids, block)
        found = jnp.where(owner == q, at, jnp.where(owner == far[s], at + kept, -1))
        return jnp.where(inside, found, -1)

    def fill_hits(s, group, first):
        slot[s] = slots_of(s, *((0, 1) if first else ((2, 3), (4, 5))[s]))

        def tile(t, carry):
            base = pl.multiple_of(t * LANES, LANES)
            row = lax.broadcasted_iota(jnp.int32, (LANES, both), 0) + base
            found = jnp.where(row == slot[s], 1.0, 0.0)
            hit[group, pl.ds(base, LANES), :] = found.astype(jnp.bfloat16)
            if s == 0:
                count = jnp.broadcast_to(jnp.sum(found, axis=1, keepdims=True), (LANES, LANES))
                at = pl.ds(base, LANES)
                cnt[at, :] = count if first else cnt[at, :] + count
            return carry

        lax.fori_loop(0, 2 * kept // LANES, tile, 0)

    def own_dots(s):
        def tile(t, carry):
            at = pl.ds(pl.multiple_of(t * kept, kept), kept)
            acc[s, at, :] = jnp.dot(
                hit[s, at, :], p2[:, s * side_w : (s + 1) * side_w], preferred_element_type=jnp.float32
            )
            return carry

        lax.fori_loop(0, 2, tile, 0)

    def near_dot(s, p, half):
        at, cols = pl.ds(half * kept, kept), pl.ds(p * part, part)
        acc[s, at, cols] += jnp.dot(hit[s, at, :], pn[s, p], preferred_element_type=jnp.float32)

    def rows_of(t):
        return pl.ds(pl.multiple_of(t * block, block), block)

    def half_rows_of(t):
        return pl.ds(pl.multiple_of(t * (block // 2), block // 2), block // 2)

    def step_b(p):
        for s in range(2):
            pts_copy(s, p).wait_recv()
            fwd_copy(s, p).start()
        for s in range(2):
            fwd_copy(s, p).wait_recv()
            near_dot(s, p, 1)

            def tile(t, carry, s=s):
                at = pl.ds(pl.multiple_of(kept + t * block, block), block)
                count = cnt[at, 0:1] if s == 0 and p == 0 else None
                asend[s, p, half_rows_of(t), :] = encode(acc[s, at, p * part : (p + 1) * part], count)
                return carry

            lax.fori_loop(0, z_n, tile, 0)
            a_copy(s, p).start()
        for s in range(2):
            near_dot(s, p, 0)

    def step_c(p):
        for s in range(2):
            a_copy(s, p).wait_recv()

            def tile(t, carry, s=s):
                at = rows_of(t)
                more, count = decode(arecv[s, p, half_rows_of(t), :])
                v = acc[s, at, p * part : (p + 1) * part] + more
                acc[s, at, p * part : (p + 1) * part] = v
                if s == 0 and p == 0:
                    total = cnt[at, 0:1] + count
                    cnt[at, :] = jnp.broadcast_to(total, (block, LANES))
                else:
                    total = None
                zsend[p, t, s * (block // 2) : (s + 1) * (block // 2), :] = encode(v, total)
                return carry

            lax.fori_loop(0, z_n, tile, 0)
        for k in range(1, z_n):
            z_copy(p, k).start()

    def xcopy(p, n, to_q):
        at = out_ref.at[p, n * PLANE + to_q]
        return remote(at, at, xs.at[p, n], xr.at[p, n], (z, nx, m))

    def ycopy(p, n, to_q):
        at = out_ref.at[p, n * PLANE + to_q]
        return remote(at, at, ys.at[p, n], yr.at[p, n], (z, ny, m))

    def dcopy(p, n, by_x):
        at = out_ref.at[p, n * PLANE + (nx if by_x else ny)]
        return remote(at, at, ds_.at[p, n], dr.at[p, n], (z, ny if by_x else nx, m))

    def gright(p, n):
        at = out_ref.at[p, n * PLANE + q]
        return remote(at, at, grs.at[p, n], grr.at[p, n], (up, q, m))

    def gleft(p, n):
        at = out_ref.at[p, n * PLANE + q]
        return remote(at, at, gls.at[p, n], glr.at[p, n], (down, q, m))

    def step_d(p):
        mine = rows_of(z)
        for k in range(1, z_n):
            z_copy(p, k).wait_recv()
        if p == 0:
            load_prior.wait()
        fresh = []
        for s in range(2):
            total = acc[s, mine, p * part : (p + 1) * part]
            count = cnt[mine, 0:1]
            for k in range(1, z_n):
                more, extra = decode(zrecv[p, k, s * (block // 2) : (s + 1) * (block // 2), :])
                total = total + more
                count = count + extra
            if p == 0 and s == 0:
                cnt[mine, :] = jnp.broadcast_to(count, (block, LANES))
            count = cnt[mine, 0:1]
            lo = s * side_w + p * part
            fallback = prior[:, lo : lo + part].astype(jnp.float32)
            fresh.append(jnp.where(count > 0.5, total / jnp.maximum(count, 1.0), fallback))
        top = jnp.max(jnp.maximum(jnp.abs(fresh[0]), jnp.abs(fresh[1])), axis=1, keepdims=True)
        power = power_of(top)
        word = power.astype(jnp.int32) + BIAS
        out_ref[p, own, : block // 2] = pack(embed(quantize(fresh[0], power), word))
        out_ref[p, own, block // 2 :] = pack(quantize(fresh[1], power))

        @pl.when(z < last)
        def _():
            gright(p, z).start()

        @pl.when(z > 0)
        def _():
            gleft(p, z).start()

        xcopy(p, z, q).start()
        ycopy(p, z, q).start()

    def relay(p, n, by_x):
        if by_x:
            xcopy(p, n, nx).wait_recv()
        else:
            ycopy(p, n, ny).wait_recv()
        dcopy(p, n, by_x).start()

    def settle(p, n, by_x):
        if by_x:
            ycopy(p, n, ny).wait_recv()
        else:
            xcopy(p, n, nx).wait_recv()
        dcopy(p, n, by_x).wait_recv()

    def each(p, k, action):
        if k == 0:
            action(p, z, p % 2 == 0)
            return

        @pl.when(z >= k)
        def _():
            action(p, z - k, (k + p) % 2 == 0)

        @pl.when(z + k <= last)
        def _():
            action(p, z + k, (k + p) % 2 == 1)

    def spread(p, k):
        @pl.when(z >= k)
        def _():
            gright(p, z - k).wait_recv()

            @pl.when(z < last)
            def _():
                gright(p, z - k).start()

            xcopy(p, z - k, q).start()
            ycopy(p, z - k, q).start()

        @pl.when(z + k <= last)
        def _():
            gleft(p, z + k).wait_recv()

            @pl.when(z > 0)
            def _():
                gleft(p, z + k).start()

            xcopy(p, z + k, q).start()
            ycopy(p, z + k, q).start()

    def lowest(i, n):
        if i == 0:
            load_c.wait()

        def tile(t, best):
            tile_ref = cents[pl.ds(pl.multiple_of(t * CTILE, CTILE), CTILE), :]
            wide = tile_ref.astype(jnp.float32)
            sq = jnp.sum(wide * wide, axis=1, keepdims=True)
            inner = lax.dot_general(
                tile_ref, p2[...], (((1,), (1,)), ((), ())), preferred_element_type=jnp.float32
            )
            return jnp.minimum(best, jnp.min(sq - 2.0 * inner, axis=0, keepdims=True))

        start = jnp.full((1, both), jnp.inf, jnp.float32) if i == 0 else low[...]
        low[...] = lax.fori_loop(i * n, (i + 1) * n, tile, start)

    low_copy = remote(low.at[:, pl.ds(rows, rows)], lowr, lo_s, lo_r, (z, q, other))

    def finish_cost():
        low_copy.wait_recv()
        wide = p2[pl.ds(0, rows), :].astype(jnp.float32)
        sq = jnp.sum(wide * wide, axis=1, keepdims=True)
        flat = jnp.broadcast_to(sq, (rows, LANES)).T[0:1, :]
        cost_ref[...] = (flat + jnp.minimum(low[:, :rows], lowr[...])) / width

    mate_copy.wait_recv()
    for s in range(2):
        fill_hits(s, s, True)
        own_dots(s)
    for s in range(2):
        fill_hits(s, s, False)

    tasks = [(i, step_b, (i,)) for i in range(pairs - 1)]
    tasks += [(2.5 + i, step_c, (i,)) for i in range(pairs)]
    tasks += [(2.7, lambda: [pts_copy(s, pairs - 1).start() for s in range(2)], ())]
    tasks[-1] = (0.5, tasks[-1][1], ())
    tasks += [(3.2, step_b, (pairs - 1,))]
    pieces = shard_rows // CTILE // 2
    for p in range(pairs):
        base = (4.8, 6, 8, 10)[p]
        tasks.append((base, step_d, (p,)))
        for k in range(1, z_n):
            tasks.append((base + 1.2 * k, spread, (p, k)))
        for k in range(z_n):
            tasks.append((base + 1.2 * k + 1.0, each, (p, k, relay)))
            tasks.append((100 + p + 0.01 * k, each, (p, k, settle)))
    for i in range(pieces):
        tasks.append((5.55 + i, lowest, (i, 2)))
    tasks.append((5.6 + pieces, low_copy.start, ()))
    tasks.append((8.7 + pieces, finish_cost, ()))
    for _, action, args in sorted(tasks, key=lambda task: task[0]):
        action(*args)

    for copy in id_copies + [mate_copy, low_copy]:
        copy.wait_send()
    for p in range(pairs):
        for s in range(2):
            pts_copy(s, p).wait_send()
            fwd_copy(s, p).wait_send()
            a_copy(s, p).wait_send()
        for t in range(z_n):
            if t > 0:
                z_copy(p, t).wait_send()

            @pl.when((z >= t) & (z < last))
            def _(p=p, t=t):
                gright(p, t).wait_send()

            @pl.when((z <= t) & (z > 0))
            def _(p=p, t=t):
                gleft(p, t).wait_send()

            xcopy(p, t, q).wait_send()
            ycopy(p, t, q).wait_send()
            dcopy(p, t, True).wait_send()


def decode_kernel(pairs, in_ref, out_ref):
    owners, block = in_ref.shape[1], in_ref.shape[2]
    half = block // 2
    side_w = out_ref.shape[1] // 2
    part = side_w // pairs
    for o in range(owners):
        at = slice(o * block, (o + 1) * block)
        for p in range(pairs):
            first = unpack(in_ref[p, o, :half])
            scale = scale_of(word_of(first))
            out_ref[at, p * part : (p + 1) * part] = first.astype(jnp.float32) * scale
            second = unpack(in_ref[p, o, half:])
            out_ref[at, side_w + p * part : side_w + (p + 1) * part] = second.astype(jnp.float32) * scale


def shards(points, centroids, assign, keep_mask):
    rows, width = points.shape
    shard_rows = centroids.shape[0]
    z_n = lax.axis_size("z")
    dp_n = z_n * PLANE
    block = shard_rows // dp_n
    kept = z_n * block
    part = LANES
    side_w = width // 2
    pairs = side_w // part
    vmem = pl.BlockSpec(memory_space=pltpu.VMEM)
    hbm = pl.BlockSpec(memory_space=pl.ANY)
    dma = pltpu.SemaphoreType.DMA
    by_pair = dma((2, pairs))
    by_z = dma((pairs, z_n))
    back, cost = pl.pallas_call(
        functools.partial(update_kernel, z_n, pairs),
        out_shape=(
            jax.ShapeDtypeStruct((pairs, dp_n, block, part), jnp.int32),
            jax.ShapeDtypeStruct((1, rows), jnp.float32),
        ),
        in_specs=[hbm, hbm, vmem, vmem],
        out_specs=(vmem, vmem),
        scratch_shapes=[
            pltpu.VMEM((2 * rows, width), points.dtype),
            pltpu.VMEM((shard_rows, width), centroids.dtype),
            pltpu.VMEM((block, width), centroids.dtype),
            pltpu.VMEM((6, 1, rows), jnp.int32),
            pltpu.VMEM((2, 1, 2 * rows), jnp.int32),
            pltpu.VMEM((2, 2 * kept, 2 * rows), jnp.bfloat16),
            pltpu.VMEM((2, pairs, 2 * rows, part), points.dtype),
            pltpu.VMEM((2, 2 * kept, side_w), jnp.float32),
            pltpu.VMEM((2 * kept, LANES), jnp.float32),
            pltpu.VMEM((2, pairs, kept // 2, part), jnp.int32),
            pltpu.VMEM((2, pairs, kept // 2, part), jnp.int32),
            pltpu.VMEM((pairs, z_n, block, part), jnp.int32),
            pltpu.VMEM((pairs, z_n, block, part), jnp.int32),
            pltpu.VMEM((1, 2 * rows), jnp.float32),
            pltpu.VMEM((1, rows), jnp.float32),
            dma((3,)), dma((5,)), dma((5,)), dma, dma,
            by_pair, by_pair, by_pair, by_pair, by_pair, by_pair,
            by_z, by_z, by_z, by_z, by_z, by_z, by_z, by_z, by_z, by_z, by_z, by_z,
            dma, dma,
        ],
        compiler_params=pltpu.CompilerParams(
            collective_id=0, has_side_effects=True, vmem_limit_bytes=40 * 1024 * 1024
        ),
        cost_estimate=pl.CostEstimate(
            flops=0, bytes_accessed=200 * 1024 * 1024, transcendentals=0
        ),
        name="update",
    )(points, centroids, assign.reshape(1, rows), keep_mask.reshape(1, rows))
    owners = max(1, min(dp_n, 512 // block))
    new_centroids = pl.pallas_call(
        functools.partial(decode_kernel, pairs),
        grid=(dp_n // owners,),
        in_specs=[pl.BlockSpec((pairs, owners, block, part), lambda i: (0, i, 0, 0))],
        out_specs=pl.BlockSpec((owners * block, width), lambda i: (i, 0)),
        out_shape=jax.ShapeDtypeStruct((shard_rows, width), jnp.float32),
        cost_estimate=pl.CostEstimate(
            flops=0, bytes_accessed=12 * 1024 * 1024, transcendentals=0
        ),
        name="decode",
    )(back)
    return new_centroids, cost.reshape(rows)


def solution(mesh):
    dp, mp = mesh.shape["dp"], mesh.shape["mp"]
    grid = Mesh(mesh.devices.reshape(dp // PLANE, PLANE, mp), ("z", "q", "mp"))
    rows = ("z", "q", "mp")
    in_specs = (P(rows, None), P("mp", None), P(rows), P(rows))
    out_specs = (P("mp", None), P(rows))
    return jax.shard_map(shards, mesh=grid, in_specs=in_specs, out_specs=out_specs, check_vma=False)
```

time: 143 us -> 107 us (0.75); the launches traced: 141 us -> 106 us
  Pallas kernels: 125 us -> 98.4 us
  other arithmetic: 12.4 us -> 0 us
  local copies, waits for them, and re-layouts: 2.99 us -> 7.27 us
    pallas_call x1 -> x2, Pallas kernels: 125 us -> 98.4 us  [the longest x1 91.5 us: shards(): pl.pallas_call(functools.partial(update_kernel, z_n, pairs), out_shape=(j...]
    unnamed x0 -> x11, local copies, waits for them, and re-layouts: none -> 7.27 us
    concatenate x1 -> x0, other arithmetic: 4.06 us -> none  [shards(): new_centroids = jnp.concatenate(pieces, axis=2).reshape(shard_rows, width)]
    convert_element_type x1 -> x0, other arithmetic: 3.37 us -> none  [shards(): pieces += [(codes[c] >> 16) * scale[c], (codes[c] << 16 >> 16) * scale[c]]]
    dynamic_slice x1 -> x0, local copies, waits for them, and re-layouts: 1.67 us -> none  [shards(): prior = lax.dynamic_slice_in_dim(centroids, own * block, block, 0)]
    div x2 -> x0, other arithmetic: 1.52 us -> none  [the longest x1 0.93 us: shards(): scale = (jnp.exp2(powers) / STEPS)[:, :, :, None]]
    reduce_sum x1 -> x0, other arithmetic: 1.5 us -> none  [shards(): point_sq = jnp.sum(point_f * point_f, axis=1)]
where the time goes in v1:
time: 107 us; the launch traced here: 106 us
  Pallas kernels  98.4 us (92%)
  local copies, waits for them, and re-layouts  7.27 us (7%)
    pallas_call x1, Pallas kernels, shards(): pl.pallas_call(functools.partial(update_kernel, z_n, pairs), out_shape=(j...  91.5 us
    unnamed x11, local copies, waits for them, and re-layouts  7.27 us
    pallas_call x1, Pallas kernels, shards(): pl.pallas_call(functools.partial(decode_kernel, pairs), grid=(dp_n // own...  6.88 us

profile of v1, /device:TPU:0, one launch (start us, length us, event | category | flops | bytes accessed | tf_op | source)
XLA Modules:
  0.0 106.3 jit_solution(11894095229995360823)
XLA Ops:
  0.6 0.0 copy-start.1
  0.6 2.2 %copy-done.1 = bf16[2048,1024]{1,0:T(8,128)(2,1)S(1)} copy-done((bf16[2048,1024]{1,0:T(8,128)(2,1)S(1)}, bf16[2048,1024]{1,0:T(8,128)(2,1)}, u32[]{:S(2)}) %copy-start.1) | copy-done | bytes 4194328
  2.8 0.0 copy-start.2
  2.8 1.2 %copy-done.2 = bf16[512,1024]{1,0:T(8,128)(2,1)S(1)} copy-done((bf16[512,1024]{1,0:T(8,128)(2,1)S(1)}, bf16[512,1024]{1,0:T(8,128)(2,1)}, u32[]{:S(2)}) %copy-start.2) | copy-done | bytes 1048600
  4.0 0.0 copy-start.3
  4.0 0.7 copy-done.3
  4.7 0.0 copy-start.4
  4.7 0.7 copy-done.4
  5.4 91.5 %update.1 = (s32[4,16,128,128]{3,2,1,0:T(8,128)S(1)}, f32[1,512]{1,0:T(1,128)S(1)}) custom-call(bf16[512,1024]{1,0:T(8,128)(2,1)S(1)} %copy-done.2, bf16[2048,1024]{1,0:T(8,128)(2,1)S(1)} %copy-done.1, s32[1,512]{1,0:T(1,128)S(1)} %bitcast.3, s32[1,512]{1,0:T(1,128)S(1)} %bitcast.4), custom_call_target="tpu_custom_call" | custom-call | bytes 209715200 | tf_op jit(solution)/shard_map/update/pallas_call | solution.py:449
  96.9 0.0 copy-start
  96.9 1.9 %copy-done = s32[4,16,128,128]{3,2,1,0:T(8,128)} copy-done((s32[4,16,128,128]{3,2,1,0:T(8,128)}, s32[4,16,128,128]{3,2,1,0:T(8,128)S(1)}, u32[]{:S(2)}) %copy-start) | copy-done | bytes 4194328
  98.9 6.9 %decode.1 = f32[2048,1024]{1,0:T(8,128)} custom-call(s32[4,16,128,128]{3,2,1,0:T(8,128)} %copy-done), custom_call_target="tpu_custom_call" | custom-call | bytes 12582912 | tf_op jit(solution)/shard_map/decode/pallas_call | solution.py:487
  105.7 0.6 copy.7
Async XLA Ops:
  0.6 2.2 %copy-start.1 = (bf16[2048,1024]{1,0:T(8,128)(2,1)S(1)}, bf16[2048,1024]{1,0:T(8,128)(2,1)}, u32[]{:S(2)}) copy-start(bf16[2048,1024]{1,0:T(8,128)(2,1)} %c_hbm.1) | copy-start | bytes 12582916
  2.8 1.2 %copy-start.2 = (bf16[512,1024]{1,0:T(8,128)(2,1)S(1)}, bf16[512,1024]{1,0:T(8,128)(2,1)}, u32[]{:S(2)}) copy-start(bf16[512,1024]{1,0:T(8,128)(2,1)} %p_hbm.1) | copy-start | bytes 3145732
  4.0 0.7 copy-start.3
  4.7 0.7 copy-start.4
  96.9 1.9 %copy-start = (s32[4,16,128,128]{3,2,1,0:T(8,128)}, s32[4,16,128,128]{3,2,1,0:T(8,128)S(1)}, u32[]{:S(2)}) copy-start(s32[4,16,128,128]{3,2,1,0:T(8,128)S(1)} %get-tuple-element.4.in_ref) | copy-start | bytes 12582916

commit v2 on v1

v2 whole, which is shorter than its diff:
```python
import functools

import jax
import jax.numpy as jnp
from jax import lax
from jax.experimental import pallas as pl
from jax.experimental.pallas import tpu as pltpu
from jax.sharding import Mesh
from jax.sharding import PartitionSpec as P

STEPS = 32000.0
TINY = 2.0**-100
BIAS = 128
EXP = 8
WORD = 32
GROUP = 16
FINE = 8.0
FINE_BIAS = 1024
FINE_BITS = 12
PLANE = 4
LATE = 2
LANES = 128
CTILE = 256
MESH = pl.DeviceIdType.MESH


def remote(src, dst, send, recv, device):
    return pltpu.make_async_remote_copy(
        src_ref=src, dst_ref=dst, send_sem=send, recv_sem=recv, device_id=device, device_id_type=MESH
    )


def power_of(top):
    return jnp.ceil(jnp.log2(jnp.maximum(top, TINY)))


def quantize(v, power):
    return jnp.floor(v * (jnp.exp2(-power) * STEPS) + 0.5).astype(jnp.int32)


def embed(code, power, count=None):
    lane = lax.broadcasted_iota(jnp.int32, code.shape, 1)
    bit = lax.shift_right_logical(jnp.broadcast_to(power, code.shape), jnp.minimum(lane, 31)) & 1
    used = EXP
    if count is not None:
        at = jnp.clip(lane - EXP, 0, 31)
        bit = jnp.where(lane < EXP, bit, lax.shift_right_logical(jnp.broadcast_to(count, code.shape), at) & 1)
        used = WORD
    return (code & jnp.where(lane < used, -2, -1)) | bit


def pack(code):
    half = code.shape[0] // 2
    return (code[:half] << 16) | (code[half:] & 0xFFFF)


def unpack(packed):
    return jnp.concatenate([packed >> 16, (packed << 16) >> 16], axis=0)


def bits_word(code, lo, hi):
    lane = lax.broadcasted_iota(jnp.int32, (1, LANES), 1)
    weight = jnp.where((lane >= lo) & (lane < hi), 1 << jnp.clip(lane - lo, 0, hi - lo), 0)
    bits = (code[:, :LANES] & 1).astype(jnp.float32)
    return jnp.sum(bits * weight.astype(jnp.float32), axis=1, keepdims=True)


def scale_of(code):
    return jnp.exp2(bits_word(code, 0, EXP) - BIAS) * (1.0 / STEPS)


def count_of(code):
    return bits_word(code, EXP, WORD)


def encode(v, count=None):
    power = power_of(jnp.max(jnp.abs(v), axis=1, keepdims=True))
    if count is not None:
        count = count.astype(jnp.int32)
    return pack(embed(quantize(v, power), power.astype(jnp.int32) + BIAS, count))


def decode(packed):
    code = unpack(packed)
    return code.astype(jnp.float32) * scale_of(code)


def group_of(half):
    return min(GROUP, half)


def publish_code(v):
    half = v.shape[0] // 2
    size = group_of(half)
    lane = lax.broadcasted_iota(jnp.int32, (size, LANES), 1)
    out = []
    for g in range(half // size):
        hi, lo = v[g * size : (g + 1) * size], v[half + g * size : half + (g + 1) * size]
        top = jnp.max(jnp.maximum(jnp.abs(hi), jnp.abs(lo)), axis=0, keepdims=True)
        top = jnp.maximum(jnp.max(top, axis=1, keepdims=True), TINY)
        word = jnp.ceil(jnp.log2(top) * FINE)
        factor = jnp.exp2(word * (-1.0 / FINE)) * STEPS
        codes = [jnp.floor(part * factor + 0.5).astype(jnp.int32) for part in (hi, lo)]
        bit = lax.shift_right_logical(
            jnp.broadcast_to(word.astype(jnp.int32) + FINE_BIAS, (size, LANES)), jnp.minimum(lane, 31)
        ) & 1
        first = (codes[0] & jnp.where(lane < FINE_BITS, -2, -1)) | jnp.where(lane < FINE_BITS, bit, 0)
        out.append((first << 16) | (codes[1] & 0xFFFF))
    return jnp.concatenate(out, axis=0)


TUNED = {
    (4, 4, 8): (
        0, 10, 19, 23, 34, 1, 11, 16, 30, 33, 36, 46, 56, 87, 113, 62, 77, 96, 61, 81,
        115, 70, 79, 94, 75, 84, 124, 80, 95, 119, 92, 110, 120, 2, 20, 25, 26, 41, 3, 24,
        28, 39, 40, 42, 52, 58, 78, 116, 64, 100, 122, 71, 101, 121, 72, 106, 133, 83, 103, 127,
        88, 111, 129, 98, 108, 136, 4, 27, 37, 38, 48, 5, 22, 31, 43, 47, 49, 57, 63, 67,
        130, 73, 132, 82, 97, 99, 125, 91, 123, 107, 126, 112, 134, 17, 35, 44, 50, 53, 13, 29,
        32, 51, 54, 55, 59, 68, 76, 128, 93, 131, 89, 109, 102, 117, 104, 137, 118, 135, 114, 138,
        6, 7, 18, 14, 21, 8, 12, 15, 9, 45, 60, 65, 66, 69, 74, 85, 86, 90, 105,
    ),
}


def schedule(z_n, pairs, tiles):
    times = {}
    for p in range(pairs):
        at = 9.0 + 3.0 * p
        for s in range(2):
            times["P", p, s] = 0.01 * p if p < pairs - 1 else 9.1
            times["A", p, s] = at + 0.01 * s
            times["B1", p, s] = at + 0.1 + 0.01 * s
            times["B2", p, s] = at + 0.5 + 0.01 * s
            times["C", p, s] = at + 8.0 + 0.01 * s
        times["Z", p] = at + 8.1
        steps = (z_n - 1).bit_length()
        for b in range(1, steps):
            times["H", p, b] = at + 8.0 + 5.5 * b
        done = max(26.0 + 4.0 * p, at + 8.0 + 5.5 * steps)
        times["D", p] = done
        if p >= pairs - LATE:
            times["F", p] = done + 3.2
        for k in range(z_n):
            for d in range(2 if k else 1):
                if k:
                    times["E", p, k, d] = done + 3.5 * k
                if p < pairs - LATE:
                    times["R", p, k, d] = done + 3.5 * k + 3.2
                times["S", p, k, d] = done + 3.5 * k + 6.8
    times["mate",] = 0.005
    for s in range(2):
        times["hitO", s] = 2.0 + 0.1 * s
        times["hitN", s] = 4.6 + 0.1 * s
        times["own", s, 1] = 4.0 + 0.1 * s
        times["own", s, 0] = 4.3 + 0.1 * s
    for i in range(tiles):
        times["L", i] = 26.5 + 1.5 * i
    times["X",] = 27.0 + 1.5 * tiles
    times["Y",] = 33.0 + 1.5 * tiles
    tuned = TUNED.get((z_n, pairs, tiles))
    if tuned is not None:
        times = dict(zip(times, tuned, strict=True))
    return sorted(times, key=lambda task: times[task])


def update_kernel(
    z_n, pairs, p_hbm, c_hbm, assign_hbm, keep_hbm, code_hbm, cost_ref,
    out_ref, p2, cents, ak, prior, idv, slot, hit, pn, acc, cnt, asend, arecv, zsend, zrecv, low, lowr,
    loc, ids_s, ids_r, mt_s, mt_r, ps, pr, fs, fr, as_, ar, zs, zr,
    grs, grr, gls, glr, xs, xr, ys, yr, ds_, dr, outs, f1s, f1r, f2s, f2r, hrs, hrr, hls, hlr, lo_s, lo_r,
):
    z, q, m = lax.axis_index("z"), lax.axis_index("q"), lax.axis_index("mp")
    nx = q + 1 - 2 * lax.rem(q, 2)
    ny = lax.rem(q + 2, PLANE)
    other = 1 - m
    rows, width = p_hbm.shape
    shard_rows = c_hbm.shape[0]
    block = prior.shape[0]
    both = 2 * rows
    kept = z_n * block
    side_w = width // 2
    part = side_w // pairs
    last = z_n - 1
    bits = last.bit_length()
    up, down = lax.rem(z + 1, z_n), lax.rem(z + last, z_n)
    own = z * PLANE + q
    near, far = (nx, ny), (ny, nx)

    load_p = pltpu.make_async_copy(p_hbm, p2.at[pl.ds(0, rows)], loc.at[0])
    load_prior = pltpu.make_async_copy(
        c_hbm.at[pl.ds(pl.multiple_of(own * block, block), block)], prior, loc.at[1]
    )
    load_c = pltpu.make_async_copy(c_hbm, cents, loc.at[2])
    load_a = pltpu.make_async_copy(assign_hbm, ak.at[0], loc.at[3])
    load_k = pltpu.make_async_copy(keep_hbm, ak.at[1], loc.at[4])
    for copy in (load_a, load_k, load_p):
        copy.start()

    barrier = pltpu.get_barrier_semaphore()
    peers = [(z, q, other), (z, nx, m), (z, nx, other), (z, ny, m), (z, ny, other)]
    greet = peers + [(lax.rem(z + k, z_n), q, m) for k in range(1, z_n)]
    for peer in greet:
        pl.semaphore_signal(barrier, inc=1, device_id=peer, device_id_type=MESH)
    load_a.wait()
    load_k.wait()
    idv[0] = jnp.where(ak[1] > 0, ak[0], -1)
    load_c.start()
    load_prior.start()
    pl.semaphore_wait(barrier, len(greet))

    def pts_copy(s, p):
        cols = pl.ds(s * side_w + p * part, part)
        return remote(
            p2.at[pl.ds(0, rows), cols], pn.at[s, pl.ds(0, rows), pl.ds(p * part, part)], ps.at[s, p], pr.at[s, p],
            (z, near[s], m),
        )

    def fwd_copy(s, p):
        return remote(
            pn.at[s, pl.ds(0, rows), pl.ds(p * part, part)], pn.at[s, pl.ds(rows, rows), pl.ds(p * part, part)], fs.at[s, p], fr.at[s, p],
            (z, q, other),
        )

    def a_copy(s, p):
        return remote(asend.at[s, p], arecv.at[s, p], as_.at[s, p], ar.at[s, p], (z, far[s], m))

    def z_copy(p, b):
        n = z_n >> (b + 1)
        at = pl.ds(z_n - 2 * n, n)
        bit = lax.rem(lax.div(z, 1 << b), 2)
        to = z + (1 << b) * (1 - 2 * bit)
        return remote(zsend.at[p, at], zrecv.at[p, at], zs.at[p, b], zr.at[p, b], (to, q, m))

    id_copies = [
        remote(idv.at[0], idv.at[k + 1], ids_s.at[k], ids_r.at[k], peer) for k, peer in enumerate(peers)
    ]
    mate_copy = remote(p2.at[pl.ds(0, rows)], p2.at[pl.ds(rows, rows)], mt_s, mt_r, (z, q, other))

    load_p.wait()
    for copy in id_copies:
        copy.start()

    def slots_of(s, a, b):
        ids = jnp.concatenate([idv[a], idv[b]], axis=1) - m * shard_rows
        inside = (ids >= 0) & (ids < shard_rows)
        ids = jnp.where(inside, ids, 0)
        owner = lax.rem(lax.div(ids, block), PLANE)
        at = lax.div(ids, block * PLANE) * block + lax.rem(ids, block)
        found = jnp.where(owner == q, at, jnp.where(owner == far[s], at + kept, -1))
        return jnp.where(inside, found, -1)

    def fill_hits(s, first):
        group = s if first else 2 + s
        slot[s] = slots_of(s, *((0, 1) if first else ((2, 3), (4, 5))[s]))

        def tile(t, carry):
            base = pl.multiple_of(t * LANES, LANES)
            row = lax.broadcasted_iota(jnp.int32, (LANES, both), 0) + base
            hit[group, pl.ds(base, LANES), :] = jnp.where(row == slot[s], 1.0, 0.0).astype(jnp.bfloat16)
            return carry

        lax.fori_loop(0, 2 * kept // LANES, tile, 0)

    ones = jnp.ones((both, LANES), jnp.bfloat16)

    def own_dot(s, half):
        at = pl.ds(half * kept, kept)
        acc[s, at, :] = jnp.dot(
            hit[s, at, :], p2[:, s * side_w : (s + 1) * side_w], preferred_element_type=jnp.float32
        )
        if s == 0:
            cnt[at, :] = jnp.dot(hit[s, at, :], ones, preferred_element_type=jnp.float32)

    def near_dot(s, p, half):
        at, cols = pl.ds(half * kept, kept), pl.ds(p * part, part)
        points = pn[s, :, p * part : (p + 1) * part]
        if s == 0 and p == 0:
            points = jnp.concatenate([points, ones], axis=1)
        more = jnp.dot(hit[2 + s, at, :], points, preferred_element_type=jnp.float32)
        acc[s, at, cols] += more[:, :part]
        if s == 0 and p == 0:
            cnt[at, :] += more[:, part:]

    def rows_of(t):
        return pl.ds(pl.multiple_of(t * block, block), block)

    def half_rows_of(t):
        return pl.ds(pl.multiple_of(t * (block // 2), block // 2), block // 2)

    def step_a(p, s):
        pts_copy(s, p).wait_recv()
        fwd_copy(s, p).start()

    def step_b(p, s):
        fwd_copy(s, p).wait_recv()
        near_dot(s, p, 1)

        def tile(t, carry):
            at = pl.ds(pl.multiple_of(kept + t * block, block), block)
            count = cnt[at, 0:1] if s == 0 and p == 0 else None
            asend[s, p, half_rows_of(t), :] = encode(acc[s, at, p * part : (p + 1) * part], count)
            return carry

        lax.fori_loop(0, z_n, tile, 0)
        a_copy(s, p).start()

    def step_b2(p, s):
        near_dot(s, p, 0)

    def side_of(s):
        return slice(s * (block // 2), (s + 1) * (block // 2))

    def target(b, j, mine):
        bit = lax.rem(lax.div(z, 1 << b), 2)
        return j * (2 << b) + lax.rem(z, 1 << b) + (bit if mine else 1 - bit) * (1 << b)

    def z_send(p, b):
        n = z_n >> (b + 1)
        for s in range(2):
            def tile(j, carry, s=s):
                at = rows_of(target(b, j, False))
                count = cnt[at, 0:1] if s == 0 and p == 0 else None
                zsend[p, z_n - 2 * n + j, side_of(s), :] = encode(acc[s, at, p * part : (p + 1) * part], count)
                return carry

            lax.fori_loop(0, n, tile, 0)
        z_copy(p, b).start()

    def gain(s, p, at, packed):
        acc[s, at, p * part : (p + 1) * part] += decode(packed)
        if s == 0 and p == 0:
            cnt[at, :] = jnp.broadcast_to(cnt[at, 0:1] + count_of(unpack(packed)), (block, LANES))

    def step_c(p, s):
        a_copy(s, p).wait_recv()

        def tile(t, carry):
            gain(s, p, rows_of(t), arecv[s, p, half_rows_of(t), :])
            return carry

        lax.fori_loop(0, z_n, tile, 0)

    def z_gain(p, b):
        n = z_n >> (b + 1)
        z_copy(p, b).wait_recv()
        for s in range(2):
            def tile(j, carry, s=s):
                gain(s, p, rows_of(target(b, j, True)), zrecv[p, z_n - 2 * n + j, side_of(s), :])
                return carry

            lax.fori_loop(0, n, tile, 0)

    def step_h(p, b):
        z_gain(p, b - 1)
        z_send(p, b)

    def xcopy(p, n, to_q):
        at = out_ref.at[p, n * PLANE + to_q]
        return remote(at, at, xs.at[p, n], xr.at[p, n], (z, nx, m))

    def ycopy(p, n, to_q):
        at = out_ref.at[p, n * PLANE + to_q]
        return remote(at, at, ys.at[p, n], yr.at[p, n], (z, ny, m))

    def dcopy(p, n, by_x):
        at = out_ref.at[p, n * PLANE + (nx if by_x else ny)]
        return remote(at, at, ds_.at[p, n], dr.at[p, n], (z, ny if by_x else nx, m))

    def gright(p, n):
        at = out_ref.at[p, n * PLANE + q]
        return remote(at, at, grs.at[p, n], grr.at[p, n], (up, q, m))

    def gleft(p, n):
        at = out_ref.at[p, n * PLANE + q]
        return remote(at, at, gls.at[p, n], glr.at[p, n], (down, q, m))

    def late(p):
        return p >= pairs - LATE

    def first_copy(p, s):
        at = out_ref.at[p, own, side_of(s)]
        return remote(at, at, f1s.at[p, s], f1r.at[p, s], (z, near[s], m))

    def second_copy(p, n, s, j):
        at = out_ref.at[p, n * PLANE + (near[s] if j else q), side_of(s)]
        i = 2 * s + j
        return remote(at, at, f2s.at[p, n, i], f2r.at[p, n, i], (z, far[s], m))

    def hright(p, n, s):
        at = out_ref.at[p, n * PLANE + near[s], side_of(s)]
        return remote(at, at, hrs.at[p, n, s], hrr.at[p, n, s], (up, q, m))

    def hleft(p, n, s):
        at = out_ref.at[p, n * PLANE + near[s], side_of(s)]
        return remote(at, at, hls.at[p, n, s], hlr.at[p, n, s], (down, q, m))

    def step_f(p):
        for s in range(2):
            first_copy(p, s).wait_recv()

        @pl.when(z < last)
        def _():
            for s in range(2):
                hright(p, z, s).start()

        @pl.when(z > 0)
        def _():
            for s in range(2):
                hleft(p, z, s).start()

        for s in range(2):
            second_copy(p, z, s, 1).start()

    def step_d(p):
        mine = rows_of(z)
        z_gain(p, bits - 1)
        if p == 0:
            load_prior.wait()
        count = cnt[mine, 0:1]
        fresh = []
        for s in range(2):
            lo = s * side_w + p * part
            total = acc[s, mine, p * part : (p + 1) * part]
            fallback = prior[:, lo : lo + part].astype(jnp.float32)
            fresh.append(jnp.where(count > 0.5, total / jnp.maximum(count, 1.0), fallback))
        for s in range(2):
            out_ref[p, own, side_of(s)] = publish_code(fresh[s])

        @pl.when(z < last)
        def _():
            gright(p, z).start()

        @pl.when(z > 0)
        def _():
            gleft(p, z).start()

        if late(p):
            for s in range(2):
                first_copy(p, s).start()
            for s in range(2):
                second_copy(p, z, s, 0).start()
            return

        xcopy(p, z, q).start()
        ycopy(p, z, q).start()

    def relay(p, n, by_x):
        if by_x:
            xcopy(p, n, nx).wait_recv()
        else:
            ycopy(p, n, ny).wait_recv()
        dcopy(p, n, by_x).start()

    def settle(p, n, by_x):
        if late(p):
            for s in range(2):
                for j in range(2):
                    second_copy(p, n, s, j).wait_recv()
            put(p, n).start()
            return
        if by_x:
            ycopy(p, n, ny).wait_recv()
        else:
            xcopy(p, n, nx).wait_recv()
        dcopy(p, n, by_x).wait_recv()

        put(p, n).start()

    def put(p, n):
        at = pl.ds(n * PLANE, PLANE)
        return pltpu.make_async_copy(out_ref.at[p, at], code_hbm.at[p, at], outs.at[p, n])

    def each(p, k, d, action):
        if k == 0:
            action(p, z, p % 2 == 0)
            return

        @pl.when((z >= k) if d == 0 else (z + k <= last))
        def _():
            action(p, z - k if d == 0 else z + k, (k + p) % 2 == d)

    def spread(p, k, d):
        @pl.when((z >= k) if d == 0 else (z + k <= last))
        def _():
            n, hop = (z - k, gright) if d == 0 else (z + k, gleft)
            hop(p, n).wait_recv()

            @pl.when((z < last) if d == 0 else (z > 0))
            def _():
                hop(p, n).start()

            if not late(p):
                xcopy(p, n, q).start()
                ycopy(p, n, q).start()
                return

            for s in range(2):
                second_copy(p, n, s, 0).start()
            hops = hright if d == 0 else hleft
            for s in range(2):
                hops(p, n, s).wait_recv()

            @pl.when((z < last) if d == 0 else (z > 0))
            def _():
                for s in range(2):
                    hops(p, n, s).start()

            for s in range(2):
                second_copy(p, n, s, 1).start()

    met = []

    def meet():
        if not met:
            met.append(True)
            mate_copy.wait_recv()

    seen = []

    def lowest():
        i = len(seen)
        seen.append(i)
        meet()
        if i == 0:
            load_c.wait()

        def tile(t, best):
            tile_ref = cents[pl.ds(pl.multiple_of(t * CTILE, CTILE), CTILE), :]
            wide = tile_ref.astype(jnp.float32)
            sq = jnp.sum(wide * wide, axis=1, keepdims=True)
            inner = lax.dot_general(
                tile_ref, p2[...], (((1,), (1,)), ((), ())), preferred_element_type=jnp.float32
            )
            return jnp.minimum(best, jnp.min(sq - 2.0 * inner, axis=0, keepdims=True))

        start = jnp.full((1, both), jnp.inf, jnp.float32) if i == 0 else low[...]
        low[...] = lax.fori_loop(i, i + 1, tile, start)

    low_copy = remote(low.at[:, pl.ds(rows, rows)], lowr, lo_s, lo_r, (z, q, other))

    def finish_cost():
        low_copy.wait_recv()
        wide = p2[pl.ds(0, rows), :].astype(jnp.float32)
        sq = jnp.sum(wide * wide, axis=1, keepdims=True)
        flat = jnp.broadcast_to(sq, (rows, LANES)).T[0:1, :]
        cost_ref[...] = (flat + jnp.minimum(low[:, :rows], lowr[...])) / width

    greeted = []

    def hits(s, first):
        if not greeted:
            greeted.append(True)
            for copy in id_copies:
                copy.wait_recv()
        fill_hits(s, first)

    def own_part(s, half):
        meet()
        own_dot(s, half)

    actions = {
        "P": lambda p, s: pts_copy(s, p).start(), "mate": mate_copy.start,
        "hitO": lambda s: hits(s, True), "hitN": lambda s: hits(s, False), "own": own_part,
        "A": step_a, "B1": step_b, "B2": step_b2, "C": step_c, "Z": lambda p: z_send(p, 0), "H": step_h,
        "D": step_d, "F": step_f, "E": spread, "R": lambda p, k, d: each(p, k, d, relay),
        "S": lambda p, k, d: each(p, k, d, settle), "L": lambda i: lowest(),
        "X": low_copy.start, "Y": finish_cost,
    }
    for task in schedule(z_n, pairs, shard_rows // CTILE):
        actions[task[0]](*task[1:])

    for copy in id_copies + [mate_copy, low_copy]:
        copy.wait_send()
    for p in range(pairs):
        for s in range(2):
            if late(p):
                first_copy(p, s).wait_send()
            pts_copy(s, p).wait_send()
            fwd_copy(s, p).wait_send()
            a_copy(s, p).wait_send()
        for t in range(z_n):
            if t < bits:
                z_copy(p, t).wait_send()

            @pl.when((z >= t) & (z < last))
            def _(p=p, t=t):
                gright(p, t).wait_send()
                if late(p):
                    for s in range(2):
                        hright(p, t, s).wait_send()

            @pl.when((z <= t) & (z > 0))
            def _(p=p, t=t):
                gleft(p, t).wait_send()
                if late(p):
                    for s in range(2):
                        hleft(p, t, s).wait_send()

            put(p, t).wait()
            if late(p):
                for s in range(2):
                    for j in range(2):
                        second_copy(p, t, s, j).wait_send()
                continue
            xcopy(p, t, q).wait_send()
            ycopy(p, t, q).wait_send()
            dcopy(p, t, True).wait_send()


def decode_kernel(in_hbm, cost_in, out_hbm, cost_out, codes, fresh, cost, ins, outs, row):
    pairs, dp_n, block, part = codes.shape
    half = block // 2
    size = group_of(half)
    side_w = fresh.shape[1] // 2
    lane = lax.broadcasted_iota(jnp.int32, (1, LANES), 1)
    weight = jnp.where(lane < FINE_BITS, 1 << jnp.minimum(lane, FINE_BITS), 0).astype(jnp.float32)
    owners = max(1, min(dp_n, 256 // block))

    def load(i):
        at = pl.ds(i * owners, owners)
        return pltpu.make_async_copy(in_hbm.at[:, at], codes.at[:, at], ins.at[i])

    def store(i):
        at = pl.ds(i * owners * block, owners * block)
        return pltpu.make_async_copy(fresh.at[at], out_hbm.at[at], outs.at[i])

    for i in range(dp_n // owners):
        load(i).start()
    take = pltpu.make_async_copy(cost_in, cost, row.at[0])
    give = pltpu.make_async_copy(cost, cost_out, row.at[1])
    take.start()

    def owner(o, carry):
        for p in range(pairs):
            for s in range(2):
                cols = slice(s * side_w + p * part, s * side_w + (p + 1) * part)
                for g in range(half // size):
                    packed = codes[p, o, s * half + g * size : s * half + (g + 1) * size]
                    bits = ((packed[:8] >> 16) & 1).astype(jnp.float32)
                    word = jnp.sum(bits * weight, axis=1, keepdims=True) - FINE_BIAS
                    scale = jnp.exp2(word * (1.0 / FINE)) * (1.0 / STEPS)
                    scale = jnp.broadcast_to(scale[0:1], (1, part))
                    at = pl.multiple_of(o * block, block) + g * size
                    fresh[pl.ds(at, size), cols] = (packed >> 16).astype(jnp.float32) * scale
                    low = ((packed << 16) >> 16).astype(jnp.float32)
                    fresh[pl.ds(at + half, size), cols] = low * scale
        return carry

    for i in range(dp_n // owners):
        load(i).wait()
        lax.fori_loop(i * owners, (i + 1) * owners, owner, 0)
        store(i).start()
    take.wait()
    give.start()
    for i in range(dp_n // owners):
        store(i).wait()
    give.wait()


def shards(points, centroids, assign, keep_mask):
    rows, width = points.shape
    shard_rows = centroids.shape[0]
    z_n = lax.axis_size("z")
    dp_n = z_n * PLANE
    block = shard_rows // dp_n
    kept = z_n * block
    part = LANES
    side_w = width // 2
    pairs = side_w // part
    vmem = pl.BlockSpec(memory_space=pltpu.VMEM)
    hbm = pl.BlockSpec(memory_space=pltpu.HBM)
    dma = pltpu.SemaphoreType.DMA
    by_pair = dma((2, pairs))
    by_z = dma((pairs, z_n))
    halves = dma((pairs, 2))
    by_half = dma((pairs, z_n, 2))
    by_quarter = dma((pairs, z_n, 4))
    codes, cost = pl.pallas_call(
        functools.partial(update_kernel, z_n, pairs),
        out_shape=(
            jax.ShapeDtypeStruct((pairs, dp_n, block, part), jnp.int32),
            jax.ShapeDtypeStruct((1, rows), jnp.float32),
        ),
        in_specs=[hbm] * 4,
        out_specs=(hbm, vmem),
        scratch_shapes=[
            pltpu.VMEM((pairs, dp_n, block, part), jnp.int32),
            pltpu.VMEM((2 * rows, width), points.dtype),
            pltpu.VMEM((shard_rows, width), centroids.dtype),
            pltpu.VMEM((2, 1, rows), jnp.int32),
            pltpu.VMEM((block, width), centroids.dtype),
            pltpu.VMEM((6, 1, rows), jnp.int32),
            pltpu.VMEM((2, 1, 2 * rows), jnp.int32),
            pltpu.VMEM((4, 2 * kept, 2 * rows), jnp.bfloat16),
            pltpu.VMEM((2, 2 * rows, side_w), points.dtype),
            pltpu.VMEM((2, 2 * kept, side_w), jnp.float32),
            pltpu.VMEM((2 * kept, LANES), jnp.float32),
            pltpu.VMEM((2, pairs, kept // 2, part), jnp.int32),
            pltpu.VMEM((2, pairs, kept // 2, part), jnp.int32),
            pltpu.VMEM((pairs, z_n, block, part), jnp.int32),
            pltpu.VMEM((pairs, z_n, block, part), jnp.int32),
            pltpu.VMEM((1, 2 * rows), jnp.float32),
            pltpu.VMEM((1, rows), jnp.float32),
            dma((5,)), dma((5,)), dma((5,)), dma, dma,
            by_pair, by_pair, by_pair, by_pair, by_pair, by_pair,
            by_z, by_z, by_z, by_z, by_z, by_z, by_z, by_z, by_z, by_z, by_z, by_z, by_z,
            halves, halves, by_quarter, by_quarter, by_half, by_half, by_half, by_half,
            dma, dma,
        ],
        compiler_params=pltpu.CompilerParams(
            collective_id=0, has_side_effects=True, vmem_limit_bytes=56 * 1024 * 1024
        ),
        cost_estimate=pl.CostEstimate(
            flops=0, bytes_accessed=200 * 1024 * 1024, transcendentals=0
        ),
        name="update",
    )(points, centroids, assign.reshape(1, rows), keep_mask.reshape(1, rows))
    new_centroids, cost = pl.pallas_call(
        decode_kernel,
        in_specs=[hbm, hbm],
        out_specs=(hbm, hbm),
        out_shape=(
            jax.ShapeDtypeStruct((shard_rows, width), jnp.float32),
            jax.ShapeDtypeStruct((1, rows), jnp.float32),
        ),
        scratch_shapes=[
            pltpu.VMEM((pairs, dp_n, block, part), jnp.int32),
            pltpu.VMEM((shard_rows, width), jnp.float32),
            pltpu.VMEM((1, rows), jnp.float32),
            dma((dp_n,)), dma((dp_n,)), dma((2,)),
        ],
        compiler_params=pltpu.CompilerParams(vmem_limit_bytes=56 * 1024 * 1024),
        name="decode",
    )(codes, cost)
    return new_centroids, cost.reshape(rows)


def solution(mesh):
    dp, mp = mesh.shape["dp"], mesh.shape["mp"]
    grid = Mesh(mesh.devices.reshape(dp // PLANE, PLANE, mp), ("z", "q", "mp"))
    rows = ("z", "q", "mp")
    in_specs = (P(rows, None), P("mp", None), P(rows), P(rows))
    out_specs = (P("mp", None), P(rows))
    return jax.shard_map(shards, mesh=grid, in_specs=in_specs, out_specs=out_specs, check_vma=False)
```

time: 107 us -> 86.4 us (0.81)
  Pallas kernels: 98.4 us -> 85.4 us
  local copies, waits for them, and re-layouts: 7.27 us -> 0 us
    pallas_call x1, Pallas kernels: 91.5 us -> 80.5 us  [shards(): pl.pallas_call(functools.partial(update_kernel, z_n, pairs), out_shape=(j...]
    unnamed x11 -> x0, local copies, waits for them, and re-layouts: 7.27 us -> none
    pallas_call x1, Pallas kernels: 6.88 us -> 4.96 us  [shards(): pl.pallas_call(decode_kernel, in_specs=[hbm, hbm], out_specs=(hbm, hbm),...]
where the time goes in v2:
time: 86.4 us; the launch traced here: 86.2 us
  Pallas kernels  85.4 us (99%)
    pallas_call x1, Pallas kernels, shards(): pl.pallas_call(functools.partial(update_kernel, z_n, pairs), out_shape=(j...  80.5 us
    pallas_call x1, Pallas kernels, shards(): pl.pallas_call(decode_kernel, in_specs=[hbm, hbm], out_specs=(hbm, hbm),...  4.96 us

profile of v2, /device:TPU:0, one launch (start us, length us, event | category | flops | bytes accessed | tf_op | source)
XLA Modules:
  0.0 86.2 jit_solution(15568699080904390485)
XLA Ops:
  0.6 80.5 %update.1 = (s32[4,16,128,128]{3,2,1,0:T(8,128)}, f32[1,512]{1,0:T(1,128)}) custom-call(bf16[512,1024]{1,0:T(8,128)(2,1)} %p_hbm.1, bf16[2048,1024]{1,0:T(8,128)(2,1)} %c_hbm.1, s32[1,512]{1,0:T(1,128)} %bitcast.3, s32[1,512]{1,0:T(1,128)} %bitcast.4), custom_call_target="tpu_custom_call" | custom-call | bytes 209715200 | tf_op jit(solution)/shard_map/update/pallas_call | solution.py:678
  81.1 5.0 %decode.1 = (f32[2048,1024]{1,0:T(8,128)}, f32[1,512]{1,0:T(1,128)}) custom-call(s32[4,16,128,128]{3,2,1,0:T(8,128)} %get-tuple-element.6.in_hbm, f32[1,512]{1,0:T(1,128)} %get-tuple-element.7.cost_in), custom_call_target="tpu_custom_call" | custom-call | tf_op jit(solution)/shard_map/decode/pallas_call | solution.py:718

commit v3 on v2

--- a/solution.py
+++ b/solution.py
@@ -111,13 +111,14 @@
 
 TUNED = {
     (4, 4, 8): (
-        0, 10, 19, 23, 34, 1, 11, 16, 30, 33, 36, 46, 56, 87, 113, 62, 77, 96, 61, 81,
-        115, 70, 79, 94, 75, 84, 124, 80, 95, 119, 92, 110, 120, 2, 20, 25, 26, 41, 3, 24,
-        28, 39, 40, 42, 52, 58, 78, 116, 64, 100, 122, 71, 101, 121, 72, 106, 133, 83, 103, 127,
-        88, 111, 129, 98, 108, 136, 4, 27, 37, 38, 48, 5, 22, 31, 43, 47, 49, 57, 63, 67,
-        130, 73, 132, 82, 97, 99, 125, 91, 123, 107, 126, 112, 134, 17, 35, 44, 50, 53, 13, 29,
-        32, 51, 54, 55, 59, 68, 76, 128, 93, 131, 89, 109, 102, 117, 104, 137, 118, 135, 114, 138,
-        6, 7, 18, 14, 21, 8, 12, 15, 9, 45, 60, 65, 66, 69, 74, 85, 86, 90, 105,
+        2, 16, 19, 25, 32, 1, 12, 17, 21, 30, 34, 42, 31, 45, 55, 68, 94, 67, 85, 118,
+        66, 110, 134, 80, 89, 137, 75, 124, 138, 90, 99, 127, 79, 101, 125, 3, 20, 23, 35, 39,
+        4, 18, 22, 26, 37, 41, 51, 38, 49, 60, 70, 140, 72, 96, 115, 73, 87, 116, 81, 111,
+        136, 82, 119, 133, 95, 102, 109, 93, 108, 141, 28, 44, 53, 57, 61, 33, 52, 54, 62, 63,
+        65, 77, 64, 76, 84, 97, 122, 100, 144, 104, 128, 106, 135, 123, 143, 114, 146, 131, 145, 9,
+        24, 27, 43, 46, 13, 29, 36, 40, 48, 47, 59, 50, 58, 71, 78, 126, 88, 121, 91, 120,
+        103, 130, 98, 139, 107, 142, 112, 129, 0, 5, 6, 7, 11, 10, 8, 14, 15, 56, 69, 74,
+        83, 86, 92, 105, 113, 117, 132,
     ),
 }
 
@@ -132,10 +133,11 @@
             times["B1", p, s] = at + 0.1 + 0.01 * s
             times["B2", p, s] = at + 0.5 + 0.01 * s
             times["C", p, s] = at + 8.0 + 0.01 * s
-        times["Z", p] = at + 8.1
         steps = (z_n - 1).bit_length()
-        for b in range(1, steps):
-            times["H", p, b] = at + 8.0 + 5.5 * b
+        for s in range(2):
+            times["Z", p, s] = at + 8.1 + 0.01 * s
+            for b in range(1, steps):
+                times["H", p, b, s] = at + 8.0 + 5.5 * b + 0.01 * s
         done = max(26.0 + 4.0 * p, at + 8.0 + 5.5 * steps)
         times["D", p] = done
         if p >= pairs - LATE:
@@ -224,12 +226,17 @@
     def a_copy(s, p):
         return remote(asend.at[s, p], arecv.at[s, p], as_.at[s, p], ar.at[s, p], (z, far[s], m))
 
-    def z_copy(p, b):
+    def side_of(s):
+        return slice(s * (block // 2), (s + 1) * (block // 2))
+
+    def z_copy(p, b, s):
         n = z_n >> (b + 1)
         at = pl.ds(z_n - 2 * n, n)
         bit = lax.rem(lax.div(z, 1 << b), 2)
         to = z + (1 << b) * (1 - 2 * bit)
-        return remote(zsend.at[p, at], zrecv.at[p, at], zs.at[p, b], zr.at[p, b], (to, q, m))
+        return remote(
+            zsend.at[p, at, side_of(s)], zrecv.at[p, at, side_of(s)], zs.at[p, b, s], zr.at[p, b, s], (to, q, m)
+        )
 
     id_copies = [
         remote(idv.at[0], idv.at[k + 1], ids_s.at[k], ids_r.at[k], peer) for k, peer in enumerate(peers)
@@ -307,24 +314,21 @@
     def step_b2(p, s):
         near_dot(s, p, 0)
 
-    def side_of(s):
-        return slice(s * (block // 2), (s + 1) * (block // 2))
-
     def target(b, j, mine):
         bit = lax.rem(lax.div(z, 1 << b), 2)
         return j * (2 << b) + lax.rem(z, 1 << b) + (bit if mine else 1 - bit) * (1 << b)
 
-    def z_send(p, b):
+    def z_send(p, b, s):
         n = z_n >> (b + 1)
-        for s in range(2):
-            def tile(j, carry, s=s):
-                at = rows_of(target(b, j, False))
-                count = cnt[at, 0:1] if s == 0 and p == 0 else None
-                zsend[p, z_n - 2 * n + j, side_of(s), :] = encode(acc[s, at, p * part : (p + 1) * part], count)
-                return carry
-
-            lax.fori_loop(0, n, tile, 0)
-        z_copy(p, b).start()
+
+        def tile(j, carry):
+            at = rows_of(target(b, j, False))
+            count = cnt[at, 0:1] if s == 0 and p == 0 else None
+            zsend[p, z_n - 2 * n + j, side_of(s), :] = encode(acc[s, at, p * part : (p + 1) * part], count)
+            return carry
+
+        lax.fori_loop(0, n, tile, 0)
+        z_copy(p, b, s).start()
 
     def gain(s, p, at, packed):
         acc[s, at, p * part : (p + 1) * part] += decode(packed)
@@ -340,19 +344,19 @@
 
         lax.fori_loop(0, z_n, tile, 0)
 
-    def z_gain(p, b):
+    def z_gain(p, b, s):
         n = z_n >> (b + 1)
-        z_copy(p, b).wait_recv()
-        for s in range(2):
-            def tile(j, carry, s=s):
-                gain(s, p, rows_of(target(b, j, True)), zrecv[p, z_n - 2 * n + j, side_of(s), :])
-                return carry
-
-            lax.fori_loop(0, n, tile, 0)
-
-    def step_h(p, b):
-        z_gain(p, b - 1)
-        z_send(p, b)
+        z_copy(p, b, s).wait_recv()
+
+        def tile(j, carry):
+            gain(s, p, rows_of(target(b, j, True)), zrecv[p, z_n - 2 * n + j, side_of(s), :])
+            return carry
+
+        lax.fori_loop(0, n, tile, 0)
+
+    def step_h(p, b, s):
+        z_gain(p, b - 1, s)
+        z_send(p, b, s)
 
     def xcopy(p, n, to_q):
         at = out_ref.at[p, n * PLANE + to_q]
@@ -413,7 +417,8 @@
 
     def step_d(p):
         mine = rows_of(z)
-        z_gain(p, bits - 1)
+        for s in range(2):
+            z_gain(p, bits - 1, s)
         if p == 0:
             load_prior.wait()
         count = cnt[mine, 0:1]
@@ -561,7 +566,7 @@
     actions = {
         "P": lambda p, s: pts_copy(s, p).start(), "mate": mate_copy.start,
         "hitO": lambda s: hits(s, True), "hitN": lambda s: hits(s, False), "own": own_part,
-        "A": step_a, "B1": step_b, "B2": step_b2, "C": step_c, "Z": lambda p: z_send(p, 0), "H": step_h,
+        "A": step_a, "B1": step_b, "B2": step_b2, "C": step_c, "Z": lambda p, s: z_send(p, 0, s), "H": step_h,
         "D": step_d, "F": step_f, "E": spread, "R": lambda p, k, d: each(p, k, d, relay),
         "S": lambda p, k, d: each(p, k, d, settle), "L": lambda i: lowest(),
         "X": low_copy.start, "Y": finish_cost,
@@ -580,7 +585,8 @@
             a_copy(s, p).wait_send()
         for t in range(z_n):
             if t < bits:
-                z_copy(p, t).wait_send()
+                for s in range(2):
+                    z_copy(p, t, s).wait_send()
 
             @pl.when((z >= t) & (z < last))
             def _(p=p, t=t):
@@ -673,6 +679,7 @@
     by_pair = dma((2, pairs))
     by_z = dma((pairs, z_n))
     halves = dma((pairs, 2))
+    by_step = dma((pairs, (z_n - 1).bit_length(), 2))
     by_half = dma((pairs, z_n, 2))
     by_quarter = dma((pairs, z_n, 4))
     codes, cost = pl.pallas_call(
@@ -703,7 +710,7 @@
             pltpu.VMEM((1, rows), jnp.float32),
             dma((5,)), dma((5,)), dma((5,)), dma, dma,
             by_pair, by_pair, by_pair, by_pair, by_pair, by_pair,
-            by_z, by_z, by_z, by_z, by_z, by_z, by_z, by_z, by_z, by_z, by_z, by_z, by_z,
+            by_step, by_step, by_z, by_z, by_z, by_z, by_z, by_z, by_z, by_z, by_z, by_z, by_z,
             halves, halves, by_quarter, by_quarter, by_half, by_half, by_half, by_half,
             dma, dma,
         ],

time: 86.4 us -> 83.3 us (0.964)
  Pallas kernels: 85.4 us -> 82.3 us
    pallas_call x1, Pallas kernels: 80.5 us -> 77.3 us  [shards(): pl.pallas_call(functools.partial(update_kernel, z_n, pairs), out_shape=(j...]
where the time goes in v3:
time: 83.3 us; the launch traced here: 83.1 us
  Pallas kernels  82.3 us (99%)
    pallas_call x1, Pallas kernels, shards(): pl.pallas_call(functools.partial(update_kernel, z_n, pairs), out_shape=(j...  77.3 us
    pallas_call x1, Pallas kernels, shards(): pl.pallas_call(decode_kernel, in_specs=[hbm, hbm], out_specs=(hbm, hbm),...  4.96 us

profile of v3, /device:TPU:0, one launch (start us, length us, event | category | flops | bytes accessed | tf_op | source)
XLA Modules:
  0.0 83.1 jit_solution(12270697854063232592)
XLA Ops:
  0.6 77.3 %update.1 = (s32[4,16,128,128]{3,2,1,0:T(8,128)}, f32[1,512]{1,0:T(1,128)}) custom-call(bf16[512,1024]{1,0:T(8,128)(2,1)} %p_hbm.1, bf16[2048,1024]{1,0:T(8,128)(2,1)} %c_hbm.1, s32[1,512]{1,0:T(1,128)} %bitcast.3, s32[1,512]{1,0:T(1,128)} %bitcast.4), custom_call_target="tpu_custom_call" | custom-call | bytes 209715200 | tf_op jit(solution)/shard_map/update/pallas_call | solution.py:685
  78.0 5.0 %decode.1 = (f32[2048,1024]{1,0:T(8,128)}, f32[1,512]{1,0:T(1,128)}) custom-call(s32[4,16,128,128]{3,2,1,0:T(8,128)} %get-tuple-element.6.in_hbm, f32[1,512]{1,0:T(1,128)} %get-tuple-element.7.cost_in), custom_call_target="tpu_custom_call" | custom-call | tf_op jit(solution)/shard_map/decode/pallas_call | solution.py:725

commit v4 on v3

--- a/solution.py
+++ b/solution.py
@@ -28,6 +28,19 @@
     return pltpu.make_async_remote_copy(
         src_ref=src, dst_ref=dst, send_sem=send, recv_sem=recv, device_id=device, device_id_type=MESH
     )
+
+
+def repeat(n, body):
+    if n <= 4:
+        for t in range(n):
+            body(t)
+    else:
+        lax.fori_loop(0, n, lambda t, carry: (body(t), carry)[1], 0)
+
+
+def span(t, size, start=0):
+    at = start + t * size
+    return pl.ds(at if isinstance(at, int) else pl.multiple_of(at, size), size)
 
 
 def power_of(top):
@@ -111,14 +124,14 @@
 
 TUNED = {
     (4, 4, 8): (
-        2, 16, 19, 25, 32, 1, 12, 17, 21, 30, 34, 42, 31, 45, 55, 68, 94, 67, 85, 118,
-        66, 110, 134, 80, 89, 137, 75, 124, 138, 90, 99, 127, 79, 101, 125, 3, 20, 23, 35, 39,
-        4, 18, 22, 26, 37, 41, 51, 38, 49, 60, 70, 140, 72, 96, 115, 73, 87, 116, 81, 111,
-        136, 82, 119, 133, 95, 102, 109, 93, 108, 141, 28, 44, 53, 57, 61, 33, 52, 54, 62, 63,
-        65, 77, 64, 76, 84, 97, 122, 100, 144, 104, 128, 106, 135, 123, 143, 114, 146, 131, 145, 9,
-        24, 27, 43, 46, 13, 29, 36, 40, 48, 47, 59, 50, 58, 71, 78, 126, 88, 121, 91, 120,
-        103, 130, 98, 139, 107, 142, 112, 129, 0, 5, 6, 7, 11, 10, 8, 14, 15, 56, 69, 74,
-        83, 86, 92, 105, 113, 117, 132,
+        0, 15, 17, 21, 31, 2, 13, 16, 26, 33, 32, 40, 34, 44, 55, 69, 92, 65, 100, 125,
+        66, 78, 131, 81, 90, 142, 76, 93, 111, 88, 120, 127, 80, 96, 137, 1, 18, 22, 35, 37,
+        3, 20, 23, 39, 41, 38, 49, 42, 54, 61, 71, 118, 72, 112, 135, 74, 102, 134, 83, 97,
+        130, 79, 94, 117, 98, 106, 129, 95, 114, 144, 25, 46, 50, 57, 60, 30, 53, 56, 63, 67,
+        64, 75, 68, 77, 86, 101, 136, 109, 132, 105, 126, 113, 139, 119, 143, 121, 145, 124, 146, 4,
+        24, 29, 43, 45, 5, 28, 36, 48, 51, 47, 59, 52, 58, 73, 82, 104, 91, 115, 87, 128,
+        103, 141, 108, 122, 107, 133, 116, 140, 6, 7, 12, 14, 19, 8, 9, 10, 11, 27, 62, 70,
+        84, 85, 89, 99, 110, 123, 138,
     ),
 }
 
@@ -289,10 +302,10 @@
             cnt[at, :] += more[:, part:]
 
     def rows_of(t):
-        return pl.ds(pl.multiple_of(t * block, block), block)
+        return span(t, block)
 
     def half_rows_of(t):
-        return pl.ds(pl.multiple_of(t * (block // 2), block // 2), block // 2)
+        return span(t, block // 2)
 
     def step_a(p, s):
         pts_copy(s, p).wait_recv()
@@ -302,13 +315,12 @@
         fwd_copy(s, p).wait_recv()
         near_dot(s, p, 1)
 
-        def tile(t, carry):
-            at = pl.ds(pl.multiple_of(kept + t * block, block), block)
+        def tile(t):
+            at = span(t, block, kept)
             count = cnt[at, 0:1] if s == 0 and p == 0 else None
             asend[s, p, half_rows_of(t), :] = encode(acc[s, at, p * part : (p + 1) * part], count)
-            return carry
-
-        lax.fori_loop(0, z_n, tile, 0)
+
+        repeat(z_n, tile)
         a_copy(s, p).start()
 
     def step_b2(p, s):
@@ -321,13 +333,12 @@
     def z_send(p, b, s):
         n = z_n >> (b + 1)
 
-        def tile(j, carry):
+        def tile(j):
             at = rows_of(target(b, j, False))
             count = cnt[at, 0:1] if s == 0 and p == 0 else None
             zsend[p, z_n - 2 * n + j, side_of(s), :] = encode(acc[s, at, p * part : (p + 1) * part], count)
-            return carry
-
-        lax.fori_loop(0, n, tile, 0)
+
+        repeat(n, tile)
         z_copy(p, b, s).start()
 
     def gain(s, p, at, packed):
@@ -338,21 +349,19 @@
     def step_c(p, s):
         a_copy(s, p).wait_recv()
 
-        def tile(t, carry):
+        def tile(t):
             gain(s, p, rows_of(t), arecv[s, p, half_rows_of(t), :])
-            return carry
-
-        lax.fori_loop(0, z_n, tile, 0)
+
+        repeat(z_n, tile)
 
     def z_gain(p, b, s):
         n = z_n >> (b + 1)
         z_copy(p, b, s).wait_recv()
 
-        def tile(j, carry):
+        def tile(j):
             gain(s, p, rows_of(target(b, j, True)), zrecv[p, z_n - 2 * n + j, side_of(s), :])
-            return carry
-
-        lax.fori_loop(0, n, tile, 0)
+
+        repeat(n, tile)
 
     def step_h(p, b, s):
         z_gain(p, b - 1, s)

time: 83.3 us -> 81.6 us (0.980)
  Pallas kernels: 82.3 us -> 80.6 us
    pallas_call x1, Pallas kernels: 77.3 us -> 75.7 us  [shards(): pl.pallas_call(functools.partial(update_kernel, z_n, pairs), out_shape=(j...]
where the time goes in v4:
time: 81.6 us; the launch traced here: 81.4 us
  Pallas kernels  80.6 us (99%)
    pallas_call x1, Pallas kernels, shards(): pl.pallas_call(functools.partial(update_kernel, z_n, pairs), out_shape=(j...  75.7 us
    pallas_call x1, Pallas kernels, shards(): pl.pallas_call(decode_kernel, in_specs=[hbm, hbm], out_specs=(hbm, hbm),...  4.96 us

profile of v4, /device:TPU:0, one launch (start us, length us, event | category | flops | bytes accessed | tf_op | source)
XLA Modules:
  0.0 81.4 jit_solution(13757874594456067235)
XLA Ops:
  0.6 75.7 %update.1 = (s32[4,16,128,128]{3,2,1,0:T(8,128)}, f32[1,512]{1,0:T(1,128)}) custom-call(bf16[512,1024]{1,0:T(8,128)(2,1)} %p_hbm.1, bf16[2048,1024]{1,0:T(8,128)(2,1)} %c_hbm.1, s32[1,512]{1,0:T(1,128)} %bitcast.3, s32[1,512]{1,0:T(1,128)} %bitcast.4), custom_call_target="tpu_custom_call" | custom-call | bytes 209715200 | tf_op jit(solution)/shard_map/update/pallas_call | solution.py:694
  76.3 5.0 %decode.1 = (f32[2048,1024]{1,0:T(8,128)}, f32[1,512]{1,0:T(1,128)}) custom-call(s32[4,16,128,128]{3,2,1,0:T(8,128)} %get-tuple-element.6.in_hbm, f32[1,512]{1,0:T(1,128)} %get-tuple-element.7.cost_in), custom_call_target="tpu_custom_call" | custom-call | tf_op jit(solution)/shard_map/decode/pallas_call | solution.py:734

commit v5 on v4

--- a/solution.py
+++ b/solution.py
@@ -629,7 +629,7 @@
     side_w = fresh.shape[1] // 2
     lane = lax.broadcasted_iota(jnp.int32, (1, LANES), 1)
     weight = jnp.where(lane < FINE_BITS, 1 << jnp.minimum(lane, FINE_BITS), 0).astype(jnp.float32)
-    owners = max(1, min(dp_n, 256 // block))
+    owners = max(1, min(dp_n, LANES // block))
 
     def load(i):
         at = pl.ds(i * owners, owners)

time: 81.6 us -> 81.3 us (level)
  no operation moved by 1% of the time
where the time goes in v5:
time: 81.3 us; the launch traced here: 81.2 us
  Pallas kernels  80.4 us (99%)
    pallas_call x1, Pallas kernels, shards(): pl.pallas_call(functools.partial(update_kernel, z_n, pairs), out_shape=(j...  75.7 us
    pallas_call x1, Pallas kernels, shards(): pl.pallas_call(decode_kernel, in_specs=[hbm, hbm], out_specs=(hbm, hbm),...  4.68 us

profile of v5, /device:TPU:0, one launch (start us, length us, event | category | flops | bytes accessed | tf_op | source)
XLA Modules:
  0.0 81.2 jit_solution(15275695896870517330)
XLA Ops:
  0.6 75.7 %update.1 = (s32[4,16,128,128]{3,2,1,0:T(8,128)}, f32[1,512]{1,0:T(1,128)}) custom-call(bf16[512,1024]{1,0:T(8,128)(2,1)} %p_hbm.1, bf16[2048,1024]{1,0:T(8,128)(2,1)} %c_hbm.1, s32[1,512]{1,0:T(1,128)} %bitcast.3, s32[1,512]{1,0:T(1,128)} %bitcast.4), custom_call_target="tpu_custom_call" | custom-call | bytes 209715200 | tf_op jit(solution)/shard_map/update/pallas_call | solution.py:694
  76.3 4.7 %decode.1 = (f32[2048,1024]{1,0:T(8,128)}, f32[1,512]{1,0:T(1,128)}) custom-call(s32[4,16,128,128]{3,2,1,0:T(8,128)} %get-tuple-element.6.in_hbm, f32[1,512]{1,0:T(1,128)} %get-tuple-element.7.cost_in), custom_call_target="tpu_custom_call" | custom-call | tf_op jit(solution)/shard_map/decode/pallas_call | solution.py:734
